TPU v7x, 256 devices: a whole 4x4x8 slice. The times are simulated.
256 devices in a mesh: dp: 8 (over x, core), expert: 32 (over y, z).
Axes of the slice: x: 4, y: 4, z: 8, core: 2. Of those that a mesh axis runs over, the one named last changes fastest.
Arguments:
- tokens: bfloat16 [4096, 5120], P('expert', 'dp'), may hold values from -6 to 6
- out_grad: bfloat16 [4096, 5120], P('expert', 'dp'), may hold values from -0.59765625 to 0.59765625
- gate_values: float32 [4096, 8], P('expert'), may hold values from 0.05 to 0.5
- route_lists: int32 [4096, 8], P('expert'), may hold values from 0 to 15, all different within a row; in each aligned block of 128 rows (0 to 127, 128 to 255, ...) at most 72 rows name the same one
- expert_pairs: int32 [16], replicated, may hold values from 0 to 15, as said below
- gate_weight: bfloat16 [32, 5120, 1024], P('expert', 'dp'), as said below
- up_weight: bfloat16 [32, 5120, 1024], P('expert', 'dp'), as said below
- down_weight: bfloat16 [32, 1024, 5120], P('expert', None, 'dp'), as said below
Outputs:
- layer_output: bfloat16 [4096, 5120], P('expert', 'dp')
- token_grad: bfloat16 [4096, 5120], P('expert', 'dp')
- gate_value_grad: float32 [4096, 8], P('expert')
- gate_weight_grad: bfloat16 [32, 5120, 1024], P('expert', 'dp')
- up_weight_grad: bfloat16 [32, 5120, 1024], P('expert', 'dp')
- down_weight_grad: bfloat16 [32, 1024, 5120], P('expert', None, 'dp')
Inputs may be any that keep to these rules, and one draw needn't show every extreme that they name: `route_lists`: each token names 8 different experts; within each aligned block of 128 tokens no expert is named by more than 72 tokens. `expert_pairs`: a permutation; pair p is made of slots p and p + 16. `gate_weight`: slots p and p + 16 hold equal matrices, those of expert expert_pairs[p]. `up_weight`: slots p and p + 16 hold equal matrices. `down_weight`: slots p and p + 16 hold equal matrices.
All inputs are finite; a program needn't handle non-finite values.
Results may differ from a plain program's by a relative error of at most 0.023.
Values may be sent and summed in bfloat16 or wider, within the bound.
A program may use at most 128 MiB of HBM per device.

v0:
```python
import jax
import jax.numpy as jnp
from jax import lax
from jax.sharding import PartitionSpec as P

HALF = 36


def partner(x, axis, distance):
    return lax.ppermute(x, axis, [(i, i ^ 1 << distance) for i in range(lax.axis_size(axis))])


def shards(
    tokens, out_grad, gate_values, route_lists, expert_pairs, gate_weight, up_weight, down_weight
):
    tok_rows, width_dev = tokens.shape
    top_count = route_lists.shape[1]
    slot_count = lax.axis_size("expert")
    pair_count = slot_count // 2
    swap_bit = slot_count.bit_length() - 2
    contract_first = (((0,), (0,)), ((), ()))
    contract_second = (((1,), (1,)), ((), ()))
    catalog = jnp.arange(pair_count, dtype=jnp.int32)
    chosen = (route_lists[:, :, None] == catalog[None, None, :]).astype(jnp.int32)
    present = jnp.sum(chosen, axis=1)
    before = jnp.cumsum(present, axis=0) - present
    position = jnp.sum(chosen * before[:, None, :], axis=2)
    owner_pair = jnp.sum(
        jnp.where(
            route_lists[:, :, None] == expert_pairs[None, None, :], catalog[None, None, :], 0
        ),
        axis=2,
    )
    is_upper = (position >= HALF).astype(jnp.int32)
    target = (owner_pair + pair_count * is_upper) * HALF + position - HALF * is_upper
    capacity = slot_count * HALF
    flat_count = tok_rows * top_count
    slot_table = (
        jnp.full((capacity,), flat_count, jnp.int32)
        .at[target.reshape(-1)]
        .set(jnp.arange(flat_count, dtype=jnp.int32))
    )
    token_of = jnp.where(slot_table < flat_count, slot_table // top_count, tok_rows)
    padded_tokens = jnp.concatenate([tokens, jnp.zeros((1, width_dev), jnp.bfloat16)], axis=0)
    scaled_cot = (
        (gate_values[:, :, None] * out_grad.astype(jnp.float32)[:, None, :])
        .astype(jnp.bfloat16)
        .reshape(flat_count, width_dev)
    )
    padded_cot = jnp.concatenate([scaled_cot, jnp.zeros((1, width_dev), jnp.bfloat16)], axis=0)
    sent_tokens = padded_tokens[token_of].reshape(slot_count, HALF, width_dev)
    sent_cot = padded_cot[slot_table].reshape(slot_count, HALF, width_dev)
    got_tokens, got_cot = (
        lax.all_to_all(sent_tokens, "expert", split_axis=0, concat_axis=0, tiled=True),
        lax.all_to_all(sent_cot, "expert", split_axis=0, concat_axis=0, tiled=True),
    )
    row_total = slot_count * HALF
    rows_in = got_tokens.reshape(row_total, width_dev)
    cot_rows = got_cot.reshape(row_total, width_dev)
    w_gate = gate_weight[0]
    w_up = up_weight[0]
    w_down = down_weight[0]
    part_gate = jnp.dot(rows_in, w_gate, preferred_element_type=jnp.float32)
    part_up = jnp.dot(rows_in, w_up, preferred_element_type=jnp.float32)
    gate_pre, up_pre = (
        lax.psum(part_gate.astype(jnp.bfloat16), "dp").astype(jnp.float32),
        lax.psum(part_up.astype(jnp.bfloat16), "dp").astype(jnp.float32),
    )
    hidden = (jax.nn.silu(gate_pre) * up_pre).astype(jnp.bfloat16)
    expert_out = jnp.dot(hidden, w_down, preferred_element_type=jnp.float32).astype(jnp.bfloat16)
    grad_down = lax.dot_general(
        hidden, cot_rows, contract_first, preferred_element_type=jnp.float32
    ).astype(jnp.bfloat16)
    back_part = lax.dot_general(
        cot_rows, w_down, contract_second, preferred_element_type=jnp.float32
    )
    hidden_grad = lax.psum(back_part.astype(jnp.bfloat16), "dp").astype(jnp.float32)
    sigmoid_gate = jax.nn.sigmoid(gate_pre)
    up_grad = (hidden_grad * gate_pre * sigmoid_gate).astype(jnp.bfloat16)
    pre_grad = (
        hidden_grad * up_pre * sigmoid_gate * (1.0 + gate_pre * (1.0 - sigmoid_gate))
    ).astype(jnp.bfloat16)
    row_input_grad = (
        lax.dot_general(pre_grad, w_gate, contract_second, preferred_element_type=jnp.float32)
        + lax.dot_general(up_grad, w_up, contract_second, preferred_element_type=jnp.float32)
    ).astype(jnp.bfloat16)
    grad_gate = lax.dot_general(
        rows_in, pre_grad, contract_first, preferred_element_type=jnp.float32
    ).astype(jnp.bfloat16)
    grad_up = lax.dot_general(
        rows_in, up_grad, contract_first, preferred_element_type=jnp.float32
    ).astype(jnp.bfloat16)
    partner_gate, partner_up, partner_down = partner(
        (grad_gate, grad_up, grad_down), "expert", swap_bit
    )
    back_out, back_grad = (
        lax.all_to_all(
            expert_out.reshape(slot_count, HALF, width_dev),
            "expert",
            split_axis=0,
            concat_axis=0,
            tiled=True,
        ),
        lax.all_to_all(
            row_input_grad.reshape(slot_count, HALF, width_dev),
            "expert",
            split_axis=0,
            concat_axis=0,
            tiled=True,
        ),
    )
    out_each = back_out.reshape(capacity, width_dev)[target].astype(jnp.float32)
    grad_each = back_grad.reshape(capacity, width_dev)[target].astype(jnp.float32)
    layer_output = jnp.sum(gate_values[:, :, None] * out_each, axis=1).astype(jnp.bfloat16)
    token_grad = jnp.sum(grad_each, axis=1).astype(jnp.bfloat16)
    inner_dots = jnp.sum(out_grad.astype(jnp.float32)[:, None, :] * out_each, axis=2)
    gate_value_grad = lax.psum(inner_dots, "dp")
    gate_weight_grad = (grad_gate.astype(jnp.float32) + partner_gate.astype(jnp.float32)).astype(
        jnp.bfloat16
    )[None]
    up_weight_grad = (grad_up.astype(jnp.float32) + partner_up.astype(jnp.float32)).astype(
        jnp.bfloat16
    )[None]
    down_weight_grad = (grad_down.astype(jnp.float32) + partner_down.astype(jnp.float32)).astype(
        jnp.bfloat16
    )[None]
    return (
        layer_output,
        token_grad,
        gate_value_grad,
        gate_weight_grad,
        up_weight_grad,
        down_weight_grad,
    )


def solution(mesh):
    placed = (
        P("expert", "dp"),
        P("expert", "dp"),
        P("expert", None),
        P("expert", None),
        P(),
        P("expert", "dp", None),
        P("expert", "dp", None),
        P("expert", None, "dp"),
    )
    return jax.shard_map(
        shards,
        mesh=mesh,
        in_specs=placed,
        out_specs=(
            P("expert", "dp"),
            P("expert", "dp"),
            P("expert", None),
            P("expert", "dp", None),
            P("expert", "dp", None),
            P("expert", None, "dp"),
        ),
        check_vma=False,
    )
```

profile of v0, /device:TPU:8, one launch (start us, length us, event | category | flops | bytes accessed | tf_op | source)
XLA Modules:
  0.0 448.8 jit_solution(12803808135160498358)
XLA Ops:
  7.2 0.9 select_reduce_fusion.1
  8.4 0.7 select_reduce_fusion
  9.6 4.3 scatter_custom_fusion
  13.9 0.9 concatenate.6
  14.9 4.5 %gather_fusion = bf16[1152,640]{1,0:T(8,128)(2,1)S(1)} fusion(bf16[129,640]{1,0:T(8,128)(2,1)S(1)} %concatenate.6, s32[2048]{0:T(1024)S(1)} %get-tuple-element.30), kind=kCustom, calls=%fused_computation | custom fusion | bytes 2953728 | tf_op jit(solution)/shard_map/gather | solution.py:51
  19.4 1.3 reshape.143
  20.7 11.9 %all-to-all-start = ((bf16[32,36,640]{2,1,0:T(8,128)(2,1)}), bf16[32,36,640]{2,1,0:T(8,128)(2,1)}, u32[]{:S(2)}, u32[]{:S(2)}) async-start(bf16[32,36,640]{2,1,0:T(8,128)(2,1)} %reshape.143), calls=%async_computation | async-start | bytes 3276800 | tf_op jit(solution)/shard_map/all_to_all | solution.py:54
  33.2 4.8 %gather_fusion.2 = bf16[1152,640]{1,0:T(8,128)(2,1)} fusion(bf16[1025,640]{1,0:T(8,128)(2,1)S(1)} %concatenate.7, s32[2048]{0:T(1024)S(1)} %get-tuple-element.29), kind=kCustom, calls=%fused_computation.2 | custom fusion | bytes 2953728 | tf_op jit(solution)/shard_map/gather | solution.py:52
  38.0 3.3 reshape.147
  41.3 29.5 %all-to-all-done = bf16[32,36,640]{2,1,0:T(8,128)(2,1)} async-done(((bf16[32,36,640]{2,1,0:T(8,128)(2,1)}), bf16[32,36,640]{2,1,0:T(8,128)(2,1)}, u32[]{:S(2)}, u32[]{:S(2)}) %all-to-all-start) | async-done | bytes 1474592 | tf_op jit(solution)/shard_map/all_to_all | solution.py:54
  70.8 8.2 %all-to-all-start.2 = ((bf16[32,36,640]{2,1,0:T(8,128)(2,1)}), bf16[32,36,640]{2,1,0:T(8,128)(2,1)S(1)}, u32[]{:S(2)}, u32[]{:S(2)}) async-start(bf16[32,36,640]{2,1,0:T(8,128)(2,1)} %reshape.147), calls=%async_computation.2 | async-start | bytes 3276800 | tf_op jit(solution)/shard_map/all_to_all | solution.py:55
  79.2 3.3 reshape.144
  82.6 5.3 %convolution_convert_fusion.1 = bf16[1152,1024]{1,0:T(8,128)(2,1)} fusion(bf16[1152,640]{1,0:T(8,128)(2,1)} %reshape.144, bf16[1,640,1024]{2,1,0:T(8,128)(2,1)} %param.14), kind=kOutput, calls=%fused_computation.22 | convolution fusion | flops 1511129088 | bytes 5144576 | tf_op jit(solution)/shard_map/dot_general | solution.py:64
  87.9 3.5 convolution_convert_fusion.2
  91.4 25.3 %all-to-all-done.2 = bf16[32,36,640]{2,1,0:T(8,128)(2,1)S(1)} async-done(((bf16[32,36,640]{2,1,0:T(8,128)(2,1)}), bf16[32,36,640]{2,1,0:T(8,128)(2,1)S(1)}, u32[]{:S(2)}, u32[]{:S(2)}) %all-to-all-start.2) | async-done | bytes 1474592 | tf_op jit(solution)/shard_map/all_to_all | solution.py:55
  116.7 1.2 reshape.148
  117.9 5.3 %convolution_convert_fusion = bf16[1152,1024]{1,0:T(8,128)(2,1)} fusion(bf16[1152,640]{1,0:T(8,128)(2,1)} %reshape.148, bf16[1,1024,640]{2,1,0:T(8,128)(2,1)} %param.15), kind=kOutput, calls=%fused_computation.21 | convolution fusion | flops 1511129088 | bytes 5144576 | tf_op jit(solution)/shard_map/dot_general | solution.py:74
  123.3 96.2 %all-reduce.5.cloned.1.call-done = (bf16[1152,1024]{1,0:T(8,128)(2,1)}, bf16[1152,1024]{1,0:T(8,128)(2,1)}, bf16[1152,1024]{1,0:T(8,128)(2,1)}) async-done(((bf16[1152,1024]{1,0:T(8,128)(2,1)}, bf16[1152,1024]{1,0:T(8,128)(2,1)}, bf16[1152,1024]{1,0:T(8,128)(2,1)}), (bf16[1152,1024]{1,0:T(8,128)(2,1)}, bf16[1152,1024]{1,0:T(8,128)(2,1)}, bf16[1152,1024]{1,0:T(8,128)(2,1)})) %all-reduce.5.cloned.1.call-update) | async-done | bytes 7077904 | tf_op jit(solution)/shard_map/psum | solution.py:67
  219.4 5.7 %fusion.3 = (bf16[1152,1024]{1,0:T(8,128)(2,1)S(1)}, bf16[1152,1024]{1,0:T(8,128)(2,1)}) fusion(bf16[1152,1024]{1,0:T(8,128)(2,1)} %get-tuple-element.22, bf16[1152,1024]{1,0:T(8,128)(2,1)} %get-tuple-element.24, bf16[1152,1024]{1,0:T(8,128)(2,1)} %get-tuple-element.23), kind=kLoop, calls=%fused_computation.14 | loop fusion | flops 18874368 | bytes 11796480 | tf_op jit(solution)/shard_map/convert_element_type | solution.py:82
  225.1 1.5 copy-done.5
  226.6 2.0 fusion.21
  228.9 0.4 copy-done.12
  229.3 2.3 fusion.10
  231.6 1.4 reshape.149
  232.9 10.2 %all-to-all-start.3 = ((bf16[32,36,640]{2,1,0:T(8,128)(2,1)}), bf16[32,36,640]{2,1,0:T(8,128)(2,1)S(1)}, u32[]{:S(2)}, u32[]{:S(2)}) async-start(bf16[32,36,640]{2,1,0:T(8,128)(2,1)} %reshape.149), calls=%async_computation.3 | async-start | bytes 3276800 | tf_op jit(solution)/shard_map/all_to_all | solution.py:104
  243.1 4.0 convolution_convert_fusion.3
  247.1 1.3 reshape.145
  248.5 32.7 %all-to-all-done.3 = bf16[32,36,640]{2,1,0:T(8,128)(2,1)S(1)} async-done(((bf16[32,36,640]{2,1,0:T(8,128)(2,1)}), bf16[32,36,640]{2,1,0:T(8,128)(2,1)S(1)}, u32[]{:S(2)}, u32[]{:S(2)}) %all-to-all-start.3) | async-done | bytes 1474592 | tf_op jit(solution)/shard_map/all_to_all | solution.py:104
  281.2 8.0 %all-to-all-start.1 = ((bf16[32,36,640]{2,1,0:T(8,128)(2,1)}), bf16[32,36,640]{2,1,0:T(8,128)(2,1)}, u32[]{:S(2)}, u32[]{:S(2)}) async-start(bf16[32,36,640]{2,1,0:T(8,128)(2,1)} %reshape.145), calls=%async_computation.1 | async-start | bytes 3276800 | tf_op jit(solution)/shard_map/all_to_all | solution.py:97
  289.2 5.6 %convolution_convert_fusion.5 = bf16[640,1024]{1,0:T(8,128)(2,1)} fusion(bf16[1152,640]{1,0:T(8,128)(2,1)S(1)} %copy-done.8, bf16[1152,1024]{1,0:T(8,128)(2,1)} %get-tuple-element.23, bf16[1152,1024]{1,0:T(8,128)(2,1)} %get-tuple-element.24), kind=kOutput, calls=%fused_computation.37 | convolution fusion | flops 1520041984 | bytes 7503872 | tf_op jit(solution)/shard_map/dot_general | solution.py:90
  294.8 2.1 collective-permute-start.1
  296.9 3.0 convolution_convert_fusion.6
  299.9 1.4 collective-permute-start
  301.3 2.2 convolution_convert_fusion.4
  303.5 2.5 collective-permute-start.2
  306.2 34.9 %collective-permute-done.1 = bf16[640,1024]{1,0:T(8,128)(2,1)} collective-permute-done((bf16[640,1024]{1,0:T(8,128)(2,1)}, bf16[640,1024]{1,0:T(8,128)(2,1)}, u32[]{:S(2)}, u32[]{:S(2)}) %collective-permute-start.1) | collective-permute-done | bytes 1310752 | tf_op jit(solution)/shard_map/ppermute | solution.py:10
  341.1 3.3 fusion.15
  344.4 24.8 %collective-permute-done = bf16[640,1024]{1,0:T(8,128)(2,1)} collective-permute-done((bf16[640,1024]{1,0:T(8,128)(2,1)}, bf16[640,1024]{1,0:T(8,128)(2,1)}, u32[]{:S(2)}, u32[]{:S(2)}) %collective-permute-start) | collective-permute-done | bytes 1310752 | tf_op jit(solution)/shard_map/ppermute | solution.py:10
  369.2 3.3 fusion.14
  372.5 23.8 %collective-permute-done.2 = bf16[1024,640]{1,0:T(8,128)(2,1)} collective-permute-done((bf16[1024,640]{1,0:T(8,128)(2,1)S(1)}, bf16[1024,640]{1,0:T(8,128)(2,1)}, u32[]{:S(2)}, u32[]{:S(2)}) %collective-permute-start.2) | collective-permute-done | bytes 1310752 | tf_op jit(solution)/shard_map/ppermute | solution.py:10
  396.3 2.7 fusion.16
  399.3 4.0 gather_fusion.3
  403.4 1.5 bitcast_reduce_fusion
  404.9 2.3 reshape.146
  407.2 5.1 %gather_fusion.1 = bf16[1024,640]{1,0:T(8,128)(2,1)} fusion(bf16[1152,640]{1,0:T(8,128)(2,1)S(1)} %reshape.146, s32[1024]{0:T(1024)S(1)} %broadcast_clamp_fusion), kind=kCustom, calls=%fused_computation.1 | custom fusion | bytes 2625536 | tf_op jit(solution)/shard_map/gather | solution.py:112
  412.4 3.3 fusion.12
  415.6 25.7 %psum.31 = f32[128,8]{1,0:T(8,128)S(1)} all-reduce(f32[128,8]{1,0:T(8,128)S(1)} %get-tuple-element.18), channel_id=1, replica_groups=mesh['dp'=8,'expert'=32] {'dp'}, use_global_device_ids=true, to_apply=%region_11.12 | all-reduce | flops 1024 | bytes 8192 | tf_op jit(solution)/shard_map/psum | solution.py:117
  441.3 0.7 copy.31
  (49 shorter events, 2.5 us)
Async XLA Ops:
  7.2 80.7 %copy-start = (bf16[1,640,1024]{2,1,0:T(8,128)(2,1)S(1)}, bf16[1,640,1024]{2,1,0:T(8,128)(2,1)}, u32[]{:S(2)}) copy-start(bf16[1,640,1024]{2,1,0:T(8,128)(2,1)} %param.13) | copy-start | bytes 3932164
  20.7 11.9 %copy-start.11 = (f32[128,8]{0,1:T(8,128)S(1)}, f32[128,8]{0,1:T(8,128)}, u32[]{:S(2)}) copy-start(f32[128,8]{0,1:T(8,128)} %param.10) | copy-start | bytes 12292
  20.7 12.1 %copy-start.10 = (bf16[128,640]{1,0:T(8,128)(2,1)S(1)}, bf16[128,640]{1,0:T(8,128)(2,1)}, u32[]{:S(2)}) copy-start(bf16[128,640]{1,0:T(8,128)(2,1)} %param.9) | copy-start | bytes 491524
  20.7 50.1 %all-to-all-start = ((bf16[32,36,640]{2,1,0:T(8,128)(2,1)}), bf16[32,36,640]{2,1,0:T(8,128)(2,1)}, u32[]{:S(2)}, u32[]{:S(2)}) async-start(bf16[32,36,640]{2,1,0:T(8,128)(2,1)} %reshape.143), calls=%async_computation | async-start | bytes 3276800 | tf_op jit(solution)/shard_map/all_to_all | solution.py:54
  70.8 45.9 %all-to-all-start.2 = ((bf16[32,36,640]{2,1,0:T(8,128)(2,1)}), bf16[32,36,640]{2,1,0:T(8,128)(2,1)S(1)}, u32[]{:S(2)}, u32[]{:S(2)}) async-start(bf16[32,36,640]{2,1,0:T(8,128)(2,1)} %reshape.147), calls=%async_computation.2 | async-start | bytes 3276800 | tf_op jit(solution)/shard_map/all_to_all | solution.py:55
  79.0 140.4 %all-reduce.5.cloned.1.call-start = ((), (), s32[]{:S(2)}) async-start(), calls=%async_computation.4 | async-start | bytes 14155776 | tf_op jit(solution)/shard_map/psum | solution.py:67
  82.6 5.3 %copy-start.7 = (bf16[1152,640]{1,0:T(8,128)(2,1)S(1)}, bf16[1152,640]{1,0:T(8,128)(2,1)}, u32[]{:S(2)}) copy-start(bf16[1152,640]{1,0:T(8,128)(2,1)} %reshape.144) | copy-start | bytes 4423684
  225.1 1.5 copy-start.5
  226.6 2.0 copy-start.2
  226.6 2.4 copy-start.3
  226.6 2.7 copy-start.12
  232.9 48.2 %all-to-all-start.3 = ((bf16[32,36,640]{2,1,0:T(8,128)(2,1)}), bf16[32,36,640]{2,1,0:T(8,128)(2,1)S(1)}, u32[]{:S(2)}, u32[]{:S(2)}) async-start(bf16[32,36,640]{2,1,0:T(8,128)(2,1)} %reshape.149), calls=%async_computation.3 | async-start | bytes 3276800 | tf_op jit(solution)/shard_map/all_to_all | solution.py:104
  248.5 40.7 %copy-start.8 = (bf16[1152,640]{1,0:T(8,128)(2,1)S(1)}, bf16[1152,640]{1,0:T(8,128)(2,1)}, u32[]{:S(2)}) copy-start(bf16[1152,640]{1,0:T(8,128)(2,1)} %reshape.144) | copy-start | bytes 4423684
  281.2 123.7 %all-to-all-start.1 = ((bf16[32,36,640]{2,1,0:T(8,128)(2,1)}), bf16[32,36,640]{2,1,0:T(8,128)(2,1)}, u32[]{:S(2)}, u32[]{:S(2)}) async-start(bf16[32,36,640]{2,1,0:T(8,128)(2,1)} %reshape.145), calls=%async_computation.1 | async-start | bytes 3276800 | tf_op jit(solution)/shard_map/all_to_all | solution.py:97
  289.2 7.7 %copy-start.6 = (bf16[1152,1024]{1,0:T(8,128)(2,1)S(1)}, bf16[1152,1024]{1,0:T(8,128)(2,1)}, u32[]{:S(2)}) copy-start(bf16[1152,1024]{1,0:T(8,128)(2,1)} %copy-done.5) | copy-start | bytes 7077892
  294.8 6.5 %copy-start.4 = (bf16[1152,1024]{1,0:T(8,128)(2,1)S(1)}, bf16[1152,1024]{1,0:T(8,128)(2,1)}, u32[]{:S(2)}) copy-start(bf16[1152,1024]{1,0:T(8,128)(2,1)} %get-tuple-element.26) | copy-start | bytes 7077892
  294.8 6.5 %copy-start.9 = (bf16[1152,640]{1,0:T(8,128)(2,1)S(1)}, bf16[1152,640]{1,0:T(8,128)(2,1)}, u32[]{:S(2)}) copy-start(bf16[1152,640]{1,0:T(8,128)(2,1)} %reshape.148) | copy-start | bytes 4423684
  294.8 46.3 %collective-permute-start.1 = (bf16[640,1024]{1,0:T(8,128)(2,1)}, bf16[640,1024]{1,0:T(8,128)(2,1)}, u32[]{:S(2)}, u32[]{:S(2)}) collective-permute-start(bf16[640,1024]{1,0:T(8,128)(2,1)} %convolution_convert_fusion.5), channel_id=1, source_target_pairs={{0,16},{1,17},{2,18},{3,19},{4,20},{5,21},{6,22},{7,23},{8,24},{9,... | collective-permute-start | bytes 3932168 | tf_op jit(solution)/shard_map/ppermute | solution.py:10
  299.9 69.3 %collective-permute-start = (bf16[640,1024]{1,0:T(8,128)(2,1)}, bf16[640,1024]{1,0:T(8,128)(2,1)}, u32[]{:S(2)}, u32[]{:S(2)}) collective-permute-start(bf16[640,1024]{1,0:T(8,128)(2,1)} %convolution_convert_fusion.6), channel_id=1, source_target_pairs={{0,16},{1,17},{2,18},{3,19},{4,20},{5,21},{6,22},{7,23},{8,24},{9,... | collective-permute-start | bytes 3932168 | tf_op jit(solution)/shard_map/ppermute | solution.py:10
  303.5 92.8 %collective-permute-start.2 = (bf16[1024,640]{1,0:T(8,128)(2,1)S(1)}, bf16[1024,640]{1,0:T(8,128)(2,1)}, u32[]{:S(2)}, u32[]{:S(2)}) collective-permute-start(bf16[1024,640]{1,0:T(8,128)(2,1)S(1)} %convolution_convert_fusion.4), channel_id=1, source_target_pairs={{0,16},{1,17},{2,18},{3,19},{4,20},{5,21},{6,22},{7,23},{8,24},{9,... | collective-permute-start | bytes 3932168 | tf_op jit(solution)/shard_map/ppermute | solution.py:10
  407.2 34.8 %copy-start.1 = (bf16[1,640,1024]{2,1,0:T(8,128)(2,1)S(1)}, bf16[1,640,1024]{2,1,0:T(8,128)(2,1)}, u32[]{:S(2)}) copy-start(bf16[1,640,1024]{2,1,0:T(8,128)(2,1)} %param.13) | copy-start | bytes 3932164
Sparse Core Ops, SparseCore 0:
  123.4 96.0 all-reduce.4
where the time goes:
time: 450 us; the launch traced here: 449 us
  waiting for transfers between devices  267 us (59%)
  starting transfers between devices  44.4 us (10%)
  local copies, waits for them, and re-layouts  42.1 us (9%)
  matrix products  33.2 us (7%)
  blocking collectives  25.7 us (6%)
  other arithmetic  21.9 us (5%)
  between operations  14.3 us (3%)
    psum x1, waiting for transfers between devices, shards(): lax.psum(part_up.astype(jnp.bfloat16), 'dp').astype(jnp.float32)  96.2 us
    ppermute x3, waiting for transfers between devices, partner(): lax.ppermute(x, axis, [(i, i ^ 1 << distance) for i in range(lax.axis_siz...  83.5 us
    all_to_all x1, waiting for transfers between devices, shards(): lax.all_to_all(row_input_grad.reshape(slot_count, HALF, width_dev), 'expe...  32.7 us
    all_to_all x1, waiting for transfers between devices, shards(): lax.all_to_all(sent_tokens, 'expert', split_axis=0, concat_axis=0, tiled=...  29.5 us
    psum x1, blocking collectives, shards(): gate_value_grad = lax.psum(inner_dots, 'dp')  25.7 us
    all_to_all x1, waiting for transfers between devices, shards(): lax.all_to_all(sent_cot, 'expert', split_axis=0, concat_axis=0, tiled=True)  25.3 us
    all_to_all x1, starting transfers between devices, shards(): lax.all_to_all(sent_tokens, 'expert', split_axis=0, concat_axis=0, tiled=...  11.9 us
    all_to_all x1, starting transfers between devices, shards(): lax.all_to_all(row_input_grad.reshape(slot_count, HALF, width_dev), 'expe...  10.2 us
  transfers between devices with their start and end apart: 8, of which 7 were waited for; matrix products, arithmetic and copies ran while one was open for 12% of the time, Pallas kernels for 0%

commit v1 on v0

--- a/solution.py
+++ b/solution.py
@@ -4,6 +4,21 @@
 from jax.sharding import PartitionSpec as P
 
 HALF = 36
+
+
+def shape_case(obj):
+    named_axis = "dp"
+    wide_n = lax.psum(1, named_axis)
+
+    def bars_cut(left_arr, out_arr):
+        if out_arr >= wide_n:
+            return left_arr
+        lower = lax.ppermute(
+            left_arr, named_axis, perm=[(dev_j, dev_j ^ out_arr) for dev_j in range(wide_n)]
+        )
+        return bars_cut(left_arr + lower, 2 * out_arr)
+
+    return bars_cut(obj, 1)
 
 
 def partner(x, axis, distance):
@@ -114,7 +129,7 @@
     layer_output = jnp.sum(gate_values[:, :, None] * out_each, axis=1).astype(jnp.bfloat16)
     token_grad = jnp.sum(grad_each, axis=1).astype(jnp.bfloat16)
     inner_dots = jnp.sum(out_grad.astype(jnp.float32)[:, None, :] * out_each, axis=2)
-    gate_value_grad = lax.psum(inner_dots, "dp")
+    gate_value_grad = shape_case(inner_dots)
     gate_weight_grad = (grad_gate.astype(jnp.float32) + partner_gate.astype(jnp.float32)).astype(
         jnp.bfloat16
     )[None]

time: 450 us -> 419 us (0.931)
  blocking collectives: 25.7 us -> 0 us
  waiting for transfers between devices: 267 us -> 256 us
  starting transfers between devices: 44.4 us -> 50.4 us
    all_to_all x1, waiting for transfers between devices: 32.7 us -> 0.01 us  [shards(): lax.all_to_all(row_input_grad.reshape(slot_count, HALF, width_dev), 'expe...]
    all_to_all x1, waiting for transfers between devices: 0.01 us -> 30.6 us  [shards(): lax.all_to_all(expert_out.reshape(slot_count, HALF, width_dev), 'expert',...]
    psum x1 -> x0, blocking collectives: 25.7 us -> none  [shards(): gate_value_grad = lax.psum(inner_dots, 'dp')]
    ppermute x3, waiting for transfers between devices: 83.5 us -> 74.3 us  [partner(): lax.ppermute(x, axis, [(i, i ^ 1 << distance) for i in range(lax.axis_siz...]
    ppermute x0 -> x3, starting transfers between devices: none -> 6.17 us  [bars_cut(): lax.ppermute(left_arr, named_axis, perm=[(dev_j, dev_j ^ out_arr) for dev...]
  transfers between devices with their start and end apart: 8 -> 11, of which waited for: 7 -> 7; matrix products, arithmetic and copies ran while one was open for 12% -> 16% of each run, Pallas kernels for 0% -> 0%
where the time goes in v1:
time: 419 us; the launch traced here: 418 us
  waiting for transfers between devices  256 us (61%)
  starting transfers between devices  50.4 us (12%)
  local copies, waits for them, and re-layouts  41.5 us (10%)
  matrix products  33.7 us (8%)
  other arithmetic  22.2 us (5%)
  between operations  14.3 us (3%)
    psum x1, waiting for transfers between devices, shards(): lax.psum(part_up.astype(jnp.bfloat16), 'dp').astype(jnp.float32)  96.2 us
    ppermute x3, waiting for transfers between devices, partner(): lax.ppermute(x, axis, [(i, i ^ 1 << distance) for i in range(lax.axis_siz...  74.3 us
    all_to_all x1, waiting for transfers between devices, shards(): lax.all_to_all(expert_out.reshape(slot_count, HALF, width_dev), 'expert',...  30.6 us
    all_to_all x1, waiting for transfers between devices, shards(): lax.all_to_all(sent_tokens, 'expert', split_axis=0, concat_axis=0, tiled=...  29.5 us
    all_to_all x1, waiting for transfers between devices, shards(): lax.all_to_all(sent_cot, 'expert', split_axis=0, concat_axis=0, tiled=True)  25.3 us
    all_to_all x1, starting transfers between devices, shards(): lax.all_to_all(sent_tokens, 'expert', split_axis=0, concat_axis=0, tiled=...  11.9 us
    all_to_all x1, starting transfers between devices, shards(): lax.all_to_all(expert_out.reshape(slot_count, HALF, width_dev), 'expert',...  10.3 us
  transfers between devices with their start and end apart: 11, of which 7 were waited for; matrix products, arithmetic and copies ran while one was open for 16% of the time, Pallas kernels for 0%

profile of v1, /device:TPU:8, one launch (start us, length us, event | category | flops | bytes accessed | tf_op | source)
XLA Modules:
  0.0 418.1 jit_solution(9133412958255246245)
XLA Ops:
  7.2 0.9 select_reduce_fusion.1
  8.4 0.7 select_reduce_fusion
  9.6 4.3 %scatter_custom_fusion = s32[1152]{0:T(1024)S(1)} fusion(s32[1024]{0:T(1024)S(1)} %bitcast.60, s32[1024]{0:T(1024)S(1)} %iota.7, s32[]{:T(128)} %constant.16.clone.1), kind=kCustom, calls=%fused_computation.77 | custom fusion | bytes 4612 | tf_op jit(solution)/shard_map/scatter | solution.py:56
  13.9 0.9 concatenate.6
  14.9 4.5 %gather_fusion = bf16[1152,640]{1,0:T(8,128)(2,1)S(1)} fusion(bf16[129,640]{1,0:T(8,128)(2,1)S(1)} %concatenate.6, s32[2048]{0:T(1024)S(1)} %get-tuple-element.30), kind=kCustom, calls=%fused_computation | custom fusion | bytes 2953728 | tf_op jit(solution)/shard_map/gather | solution.py:66
  19.4 1.4 reshape.143
  20.7 11.9 %all-to-all-start = ((bf16[32,36,640]{2,1,0:T(8,128)(2,1)}), bf16[32,36,640]{2,1,0:T(8,128)(2,1)}, u32[]{:S(2)}, u32[]{:S(2)}) async-start(bf16[32,36,640]{2,1,0:T(8,128)(2,1)} %reshape.143), calls=%async_computation | async-start | bytes 3276800 | tf_op jit(solution)/shard_map/all_to_all | solution.py:69
  33.2 4.8 %gather_fusion.2 = bf16[1152,640]{1,0:T(8,128)(2,1)} fusion(bf16[1025,640]{1,0:T(8,128)(2,1)S(1)} %concatenate.7, s32[2048]{0:T(1024)S(1)} %get-tuple-element.29), kind=kCustom, calls=%fused_computation.2 | custom fusion | bytes 2953728 | tf_op jit(solution)/shard_map/gather | solution.py:67
  38.0 3.3 reshape.147
  41.3 29.5 %all-to-all-done = bf16[32,36,640]{2,1,0:T(8,128)(2,1)} async-done(((bf16[32,36,640]{2,1,0:T(8,128)(2,1)}), bf16[32,36,640]{2,1,0:T(8,128)(2,1)}, u32[]{:S(2)}, u32[]{:S(2)}) %all-to-all-start) | async-done | bytes 1474592 | tf_op jit(solution)/shard_map/all_to_all | solution.py:69
  70.8 8.2 %all-to-all-start.2 = ((bf16[32,36,640]{2,1,0:T(8,128)(2,1)}), bf16[32,36,640]{2,1,0:T(8,128)(2,1)S(1)}, u32[]{:S(2)}, u32[]{:S(2)}) async-start(bf16[32,36,640]{2,1,0:T(8,128)(2,1)} %reshape.147), calls=%async_computation.2 | async-start | bytes 3276800 | tf_op jit(solution)/shard_map/all_to_all | solution.py:70
  79.2 3.3 reshape.144
  82.6 5.4 %convolution_convert_fusion.1 = bf16[1152,1024]{1,0:T(8,128)(2,1)} fusion(bf16[1152,640]{1,0:T(8,128)(2,1)} %reshape.144, bf16[1,640,1024]{2,1,0:T(8,128)(2,1)} %param.14), kind=kOutput, calls=%fused_computation.22 | convolution fusion | flops 1511129088 | bytes 5144576 | tf_op jit(solution)/shard_map/dot_general | solution.py:79
  87.9 3.5 convolution_convert_fusion.2
  91.4 25.3 %all-to-all-done.2 = bf16[32,36,640]{2,1,0:T(8,128)(2,1)S(1)} async-done(((bf16[32,36,640]{2,1,0:T(8,128)(2,1)}), bf16[32,36,640]{2,1,0:T(8,128)(2,1)S(1)}, u32[]{:S(2)}, u32[]{:S(2)}) %all-to-all-start.2) | async-done | bytes 1474592 | tf_op jit(solution)/shard_map/all_to_all | solution.py:70
  116.7 1.3 reshape.148
  118.0 4.9 %convolution_convert_fusion = bf16[1152,1024]{1,0:T(8,128)(2,1)} fusion(bf16[1152,640]{1,0:T(8,128)(2,1)} %reshape.148, bf16[1,1024,640]{2,1,0:T(8,128)(2,1)S(1)} %copy-done), kind=kOutput, calls=%fused_computation.21 | convolution fusion | flops 1511129088 | bytes 5144576 | tf_op jit(solution)/shard_map/dot_general | solution.py:89
  122.9 96.2 %all-reduce.5.cloned.1.call-done = (bf16[1152,1024]{1,0:T(8,128)(2,1)}, bf16[1152,1024]{1,0:T(8,128)(2,1)}, bf16[1152,1024]{1,0:T(8,128)(2,1)}) async-done(((bf16[1152,1024]{1,0:T(8,128)(2,1)}, bf16[1152,1024]{1,0:T(8,128)(2,1)}, bf16[1152,1024]{1,0:T(8,128)(2,1)}), (bf16[1152,1024]{1,0:T(8,128)(2,1)}, bf16[1152,1024]{1,0:T(8,128)(2,1)}, bf16[1152,1024]{1,0:T(8,128)(2,1)})) %all-reduce.5.cloned.1.call-update) | async-done | bytes 7077904 | tf_op jit(solution)/shard_map/psum | solution.py:82
  219.0 5.7 %fusion.3 = (bf16[1152,1024]{1,0:T(8,128)(2,1)}, bf16[1152,1024]{1,0:T(8,128)(2,1)S(1)}) fusion(bf16[1152,1024]{1,0:T(8,128)(2,1)} %get-tuple-element.22, bf16[1152,1024]{1,0:T(8,128)(2,1)} %get-tuple-element.24, bf16[1152,1024]{1,0:T(8,128)(2,1)} %get-tuple-element.23), kind=kLoop, calls=%fused_computation.14 | loop fusion | flops 18874368 | bytes 11796480 | tf_op jit(solution)/shard_map/convert_element_type | solution.py:97
  224.7 1.5 copy-done.4
  226.2 2.0 convolution_convert_fusion.3
  228.2 1.3 reshape.145
  229.6 10.3 %all-to-all-start.1 = ((bf16[32,36,640]{2,1,0:T(8,128)(2,1)}), bf16[32,36,640]{2,1,0:T(8,128)(2,1)S(1)}, u32[]{:S(2)}, u32[]{:S(2)}) async-start(bf16[32,36,640]{2,1,0:T(8,128)(2,1)} %reshape.145), calls=%async_computation.1 | async-start | bytes 3276800 | tf_op jit(solution)/shard_map/all_to_all | solution.py:112
  239.9 3.8 fusion.21
  243.8 2.3 fusion.10
  246.1 1.3 reshape.149
  247.4 30.6 %all-to-all-done.1 = bf16[32,36,640]{2,1,0:T(8,128)(2,1)S(1)} async-done(((bf16[32,36,640]{2,1,0:T(8,128)(2,1)}), bf16[32,36,640]{2,1,0:T(8,128)(2,1)S(1)}, u32[]{:S(2)}, u32[]{:S(2)}) %all-to-all-start.1) | async-done | bytes 1474592 | tf_op jit(solution)/shard_map/all_to_all | solution.py:112
  278.0 8.0 %all-to-all-start.3 = ((bf16[32,36,640]{2,1,0:T(8,128)(2,1)}), bf16[32,36,640]{2,1,0:T(8,128)(2,1)}, u32[]{:S(2)}, u32[]{:S(2)}) async-start(bf16[32,36,640]{2,1,0:T(8,128)(2,1)} %reshape.149), calls=%async_computation.3 | async-start | bytes 3276800 | tf_op jit(solution)/shard_map/all_to_all | solution.py:119
  286.0 5.6 %convolution_convert_fusion.5 = bf16[640,1024]{1,0:T(8,128)(2,1)} fusion(bf16[1152,640]{1,0:T(8,128)(2,1)S(1)} %copy-done.8, bf16[1152,1024]{1,0:T(8,128)(2,1)} %get-tuple-element.23, bf16[1152,1024]{1,0:T(8,128)(2,1)} %get-tuple-element.24), kind=kOutput, calls=%fused_computation.37 | convolution fusion | flops 1520041984 | bytes 7503872 | tf_op jit(solution)/shard_map/dot_general | solution.py:105
  291.6 2.1 collective-permute-start.4
  293.7 3.0 convolution_convert_fusion.6
  296.7 1.4 collective-permute-start.3
  298.1 3.3 convolution_convert_fusion.4
  301.4 2.1 collective-permute-start.5
  303.8 34.2 %collective-permute-done.4 = bf16[640,1024]{1,0:T(8,128)(2,1)} collective-permute-done((bf16[640,1024]{1,0:T(8,128)(2,1)}, bf16[640,1024]{1,0:T(8,128)(2,1)}, u32[]{:S(2)}, u32[]{:S(2)}) %collective-permute-start.4) | collective-permute-done | bytes 1310752 | tf_op jit(solution)/shard_map/ppermute | solution.py:25
  337.9 3.3 fusion.15
  341.5 4.0 gather_fusion.1
  345.6 1.8 fusion.12
  347.4 18.6 %collective-permute-done.3 = bf16[640,1024]{1,0:T(8,128)(2,1)} collective-permute-done((bf16[640,1024]{1,0:T(8,128)(2,1)}, bf16[640,1024]{1,0:T(8,128)(2,1)}, u32[]{:S(2)}, u32[]{:S(2)}) %collective-permute-start.3) | collective-permute-done | bytes 1310752 | tf_op jit(solution)/shard_map/ppermute | solution.py:25
  366.0 3.3 fusion.14
  369.3 2.2 collective-permute-start.1
  371.5 21.6 %collective-permute-done.5 = bf16[1024,640]{1,0:T(8,128)(2,1)} collective-permute-done((bf16[1024,640]{1,0:T(8,128)(2,1)}, bf16[1024,640]{1,0:T(8,128)(2,1)}, u32[]{:S(2)}, u32[]{:S(2)}) %collective-permute-start.5) | collective-permute-done | bytes 1310752 | tf_op jit(solution)/shard_map/ppermute | solution.py:25
  393.1 3.1 fusion.16
  396.2 2.3 reshape.150
  398.5 5.2 %gather_fusion.3 = bf16[1024,640]{1,0:T(8,128)(2,1)} fusion(bf16[1152,640]{1,0:T(8,128)(2,1)S(1)} %reshape.150, s32[1024]{0:T(1024)S(1)} %broadcast_clamp_fusion), kind=kCustom, calls=%fused_computation.3 | custom fusion | bytes 2625536 | tf_op jit(solution)/shard_map/gather | solution.py:128
  403.7 3.9 collective-permute-start.2
  407.7 2.9 bitcast_reduce_fusion
  410.6 0.7 copy.31
  (61 shorter events, 2.2 us)
Async XLA Ops:
  7.2 110.8 %copy-start = (bf16[1,1024,640]{2,1,0:T(8,128)(2,1)S(1)}, bf16[1,1024,640]{2,1,0:T(8,128)(2,1)}, u32[]{:S(2)}) copy-start(bf16[1,1024,640]{2,1,0:T(8,128)(2,1)} %param.15) | copy-start | bytes 3932164
  20.7 11.9 %copy-start.11 = (f32[128,8]{0,1:T(8,128)S(1)}, f32[128,8]{0,1:T(8,128)}, u32[]{:S(2)}) copy-start(f32[128,8]{0,1:T(8,128)} %param.10) | copy-start | bytes 12292
  20.7 12.1 %copy-start.10 = (bf16[128,640]{1,0:T(8,128)(2,1)S(1)}, bf16[128,640]{1,0:T(8,128)(2,1)}, u32[]{:S(2)}) copy-start(bf16[128,640]{1,0:T(8,128)(2,1)} %param.9) | copy-start | bytes 491524
  20.7 50.1 %all-to-all-start = ((bf16[32,36,640]{2,1,0:T(8,128)(2,1)}), bf16[32,36,640]{2,1,0:T(8,128)(2,1)}, u32[]{:S(2)}, u32[]{:S(2)}) async-start(bf16[32,36,640]{2,1,0:T(8,128)(2,1)} %reshape.143), calls=%async_computation | async-start | bytes 3276800 | tf_op jit(solution)/shard_map/all_to_all | solution.py:69
  70.8 45.9 %all-to-all-start.2 = ((bf16[32,36,640]{2,1,0:T(8,128)(2,1)}), bf16[32,36,640]{2,1,0:T(8,128)(2,1)S(1)}, u32[]{:S(2)}, u32[]{:S(2)}) async-start(bf16[32,36,640]{2,1,0:T(8,128)(2,1)} %reshape.147), calls=%async_computation.2 | async-start | bytes 3276800 | tf_op jit(solution)/shard_map/all_to_all | solution.py:70
  79.0 140.0 %all-reduce.5.cloned.1.call-start = ((), (), s32[]{:S(2)}) async-start(), calls=%async_computation.4 | async-start | bytes 14155776 | tf_op jit(solution)/shard_map/psum | solution.py:82
  82.6 5.4 %copy-start.7 = (bf16[1152,640]{1,0:T(8,128)(2,1)S(1)}, bf16[1152,640]{1,0:T(8,128)(2,1)}, u32[]{:S(2)}) copy-start(bf16[1152,640]{1,0:T(8,128)(2,1)} %reshape.144) | copy-start | bytes 4423684
  82.6 5.4 %copy-start.12 = (bf16[1,640,1024]{2,1,0:T(8,128)(2,1)S(1)}, bf16[1,640,1024]{2,1,0:T(8,128)(2,1)}, u32[]{:S(2)}) copy-start(bf16[1,640,1024]{2,1,0:T(8,128)(2,1)} %param.13) | copy-start | bytes 3932164
  224.7 1.5 copy-start.4
  229.6 10.3 %copy-start.13 = (bf16[1,640,1024]{2,1,0:T(8,128)(2,1)S(1)}, bf16[1,640,1024]{2,1,0:T(8,128)(2,1)}, u32[]{:S(2)}) copy-start(bf16[1,640,1024]{2,1,0:T(8,128)(2,1)} %param.13) | copy-start | bytes 3932164
  229.6 48.4 %all-to-all-start.1 = ((bf16[32,36,640]{2,1,0:T(8,128)(2,1)}), bf16[32,36,640]{2,1,0:T(8,128)(2,1)S(1)}, u32[]{:S(2)}, u32[]{:S(2)}) async-start(bf16[32,36,640]{2,1,0:T(8,128)(2,1)} %reshape.145), calls=%async_computation.1 | async-start | bytes 3276800 | tf_op jit(solution)/shard_map/all_to_all | solution.py:112
  239.9 3.9 copy-start.2
  239.9 3.9 copy-start.3
  239.9 3.9 copy-start.14
  247.4 38.6 %copy-start.8 = (bf16[1152,640]{1,0:T(8,128)(2,1)S(1)}, bf16[1152,640]{1,0:T(8,128)(2,1)}, u32[]{:S(2)}) copy-start(bf16[1152,640]{1,0:T(8,128)(2,1)} %reshape.144) | copy-start | bytes 4423684
  278.0 118.2 %all-to-all-start.3 = ((bf16[32,36,640]{2,1,0:T(8,128)(2,1)}), bf16[32,36,640]{2,1,0:T(8,128)(2,1)}, u32[]{:S(2)}, u32[]{:S(2)}) async-start(bf16[32,36,640]{2,1,0:T(8,128)(2,1)} %reshape.149), calls=%async_computation.3 | async-start | bytes 3276800 | tf_op jit(solution)/shard_map/all_to_all | solution.py:119
  286.0 7.7 %copy-start.6 = (bf16[1152,1024]{1,0:T(8,128)(2,1)S(1)}, bf16[1152,1024]{1,0:T(8,128)(2,1)}, u32[]{:S(2)}) copy-start(bf16[1152,1024]{1,0:T(8,128)(2,1)} %get-tuple-element.25) | copy-start | bytes 7077892
  291.6 6.5 %copy-start.5 = (bf16[1152,1024]{1,0:T(8,128)(2,1)S(1)}, bf16[1152,1024]{1,0:T(8,128)(2,1)}, u32[]{:S(2)}) copy-start(bf16[1152,1024]{1,0:T(8,128)(2,1)} %copy-done.4) | copy-start | bytes 7077892
  291.6 6.5 %copy-start.9 = (bf16[1152,640]{1,0:T(8,128)(2,1)S(1)}, bf16[1152,640]{1,0:T(8,128)(2,1)}, u32[]{:S(2)}) copy-start(bf16[1152,640]{1,0:T(8,128)(2,1)} %reshape.148) | copy-start | bytes 4423684
  291.6 46.3 %collective-permute-start.4 = (bf16[640,1024]{1,0:T(8,128)(2,1)}, bf16[640,1024]{1,0:T(8,128)(2,1)}, u32[]{:S(2)}, u32[]{:S(2)}) collective-permute-start(bf16[640,1024]{1,0:T(8,128)(2,1)} %convolution_convert_fusion.5), channel_id=1, source_target_pairs={{0,16},{1,17},{2,18},{3,19},{4,20},{5,21},{6,22},{7,23},{8,24},{9,... | collective-permute-start | bytes 3932168 | tf_op jit(solution)/shard_map/ppermute | solution.py:25
  296.7 69.3 %collective-permute-start.3 = (bf16[640,1024]{1,0:T(8,128)(2,1)}, bf16[640,1024]{1,0:T(8,128)(2,1)}, u32[]{:S(2)}, u32[]{:S(2)}) collective-permute-start(bf16[640,1024]{1,0:T(8,128)(2,1)} %convolution_convert_fusion.6), channel_id=1, source_target_pairs={{0,16},{1,17},{2,18},{3,19},{4,20},{5,21},{6,22},{7,23},{8,24},{9,... | collective-permute-start | bytes 3932168 | tf_op jit(solution)/shard_map/ppermute | solution.py:25
  301.4 91.7 %collective-permute-start.5 = (bf16[1024,640]{1,0:T(8,128)(2,1)}, bf16[1024,640]{1,0:T(8,128)(2,1)}, u32[]{:S(2)}, u32[]{:S(2)}) collective-permute-start(bf16[1024,640]{1,0:T(8,128)(2,1)} %convolution_convert_fusion.4), channel_id=1, source_target_pairs={{0,16},{1,17},{2,18},{3,19},{4,20},{5,21},{6,22},{7,23},{8,24},{9,... | collective-permute-start | bytes 3932168 | tf_op jit(solution)/shard_map/ppermute | solution.py:25
  347.4 21.9 %collective-permute-start = (f32[128,8]{1,0:T(8,128)S(1)}, f32[128,8]{1,0:T(8,128)S(1)}, u32[]{:S(2)}, u32[]{:S(2)}) collective-permute-start(f32[128,8]{1,0:T(8,128)S(1)} %get-tuple-element.18), channel_id=1, source_target_pairs={{0,32},{32,0},{64,96},{96,64},{128,160},{160,128},{192,224},{224,1... | collective-permute-start | bytes 12296 | tf_op jit(solution)/shard_map/ppermute | solution.py:16
  369.3 34.4 %collective-permute-start.1 = (f32[128,8]{1,0:T(8,128)S(1)}, f32[128,8]{1,0:T(8,128)S(1)}, u32[]{:S(2)}, u32[]{:S(2)}) collective-permute-start(f32[128,8]{1,0:T(8,128)S(1)} %add.130), channel_id=1, source_target_pairs={{0,64},{32,96},{64,0},{96,32},{128,192},{160,224},{192,128},{224,1... | collective-permute-start | bytes 12296 | tf_op jit(solution)/shard_map/ppermute | solution.py:16
  398.5 12.7 %copy-start.1 = (bf16[1,1024,640]{2,1,0:T(8,128)(2,1)S(1)}, bf16[1,1024,640]{2,1,0:T(8,128)(2,1)}, u32[]{:S(2)}) copy-start(bf16[1,1024,640]{2,1,0:T(8,128)(2,1)} %param.15) | copy-start | bytes 3932164
  403.7 6.8 %collective-permute-start.2 = (f32[128,8]{1,0:T(8,128)S(1)}, f32[128,8]{1,0:T(8,128)S(1)}, u32[]{:S(2)}, u32[]{:S(2)}) collective-permute-start(f32[128,8]{1,0:T(8,128)S(1)} %add.131), channel_id=1, source_target_pairs={{0,128},{32,160},{64,192},{96,224},{128,0},{160,32},{192,64},{224,... | collective-permute-start | bytes 12296 | tf_op jit(solution)/shard_map/ppermute | solution.py:16
Sparse Core Ops, SparseCore 0:
  123.0 96.0 all-reduce.4
